TPU v7x, 32 devices: a whole 2x2x4 slice. The times are simulated.
32 devices in a mesh: shard: 8 (over z, core), rep: 4 (over y, x).
Axes of the slice: x: 2, y: 2, z: 4, core: 2. Of those that a mesh axis runs over, the one named last changes fastest.
Arguments:
- tokens: bfloat16 [12288, 5120], P(('shard', 'rep')), may hold values from -700 to 700
- norm_gain: float32 [5120], replicated, may hold values from 0.1 to 1.9
- key_bias: float32 [1024], replicated, may hold values from -4 to 4
- key_weight: bfloat16 [8192, 1024], P('shard'), may hold values from -0.078125 to 0.078125
- cotangent: bfloat16 [12288, 1024], P(('shard', 'rep')), may hold values from -40 to 40
- block_slot: int32 [40], replicated, may hold values from 0 to 63, as said below
Outputs:
- projected: bfloat16 [12288, 1024], P(('shard', 'rep'))
- token_grad: bfloat16 [12288, 5120], P(('shard', 'rep'))
- weight_grad: float32 [8192, 1024], P('shard')
- gain_grad: float32 [5120], replicated
- bias_grad: float32 [1024], replicated
Inputs may be any that keep to these rules, and one draw needn't show every extreme that they name: Entries are distinct; block b lies on the device of shard with index block_slot[b] // 8, at its local slot block_slot[b] % 8; in every draw some device holds 8 blocks.
All inputs are finite; a program needn't handle non-finite values.
Results may differ from a plain program's by a relative error of at most 0.013.
Values may be sent and summed in bfloat16 or wider, within the bound.
A program may use at most 128 MiB of HBM per device.

v0:
```python
import jax
import jax.numpy as jnp
from jax import lax
from jax.sharding import PartitionSpec as P

BLK = 128
EPS = 1e-06


def normalize(tokens, norm_gain):
    values = tokens.astype(jnp.float32)
    inv_rms = lax.rsqrt(jnp.mean(values * values, axis=-1, keepdims=True) + EPS)
    normed = (values * inv_rms * norm_gain).astype(jnp.bfloat16)
    return (values, inv_rms, normed)


def token_backward(values, inv_rms, grad_normed, norm_gain):
    scaled = grad_normed * norm_gain
    inner = jnp.mean(scaled * values, axis=-1, keepdims=True)
    return (inv_rms * (scaled - values * inv_rms * inv_rms * inner)).astype(jnp.bfloat16)


def local(tokens, norm_gain, key_bias, key_weight, cotangent, block_slot):
    values, inv_rms, normed = normalize(tokens, norm_gain)
    row_count = tokens.shape[0]
    width = tokens.shape[1]
    local_rows = key_weight.shape[0]
    shard_count = lax.axis_size("shard")
    replicas = lax.axis_size("rep")
    slot_total = shard_count * local_rows // BLK
    block_count = width // BLK
    block_of_slot = (
        jnp.full((slot_total,), -1, jnp.int32)
        .at[block_slot]
        .set(jnp.arange(block_count, dtype=jnp.int32))
    )
    present = block_of_slot >= 0
    normed_blocks = normed.reshape(row_count, block_count, BLK)
    normed_slots = jnp.take(normed_blocks, jnp.maximum(block_of_slot, 0), axis=1)
    normed_slots = jnp.where(present[None, :, None], normed_slots, jnp.zeros((), jnp.bfloat16))
    normed_slots = normed_slots.reshape(row_count, slot_total * BLK)
    piece = lax.all_gather(key_weight, "shard", axis=0, tiled=True)
    columns = normed_slots
    forward_sum = jnp.dot(columns, piece, preferred_element_type=jnp.float32)
    backward_part = lax.dot_general(
        cotangent, piece, (((1,), (1,)), ((), ())), preferred_element_type=jnp.float32
    )
    projected = (forward_sum + key_bias).astype(jnp.bfloat16)
    grad_normed = jnp.take(backward_part.reshape(row_count, slot_total, BLK), block_slot, axis=1)
    grad_normed = grad_normed.reshape(row_count, width)
    token_grad = token_backward(values, inv_rms, grad_normed, norm_gain)
    grad_scale = float(row_count * shard_count * replicas) ** (-0.5)
    columns = normed_slots
    group_sum = lax.psum_scatter(
        (
            lax.dot_general(
                columns, cotangent, (((0,), (0,)), ((), ())), preferred_element_type=jnp.float32
            )
            * grad_scale
        ).astype(jnp.bfloat16),
        "shard",
        scatter_dimension=0,
        tiled=True,
    ).astype(jnp.float32)
    gain_part = jnp.sum(grad_normed * values * inv_rms, axis=0) * grad_scale
    bias_part = jnp.sum(cotangent.astype(jnp.float32), axis=0) * grad_scale
    weight_grad = lax.psum(group_sum, "rep")
    gain_grad, bias_grad = lax.psum((gain_part, bias_part), ("shard", "rep"))
    return (projected, token_grad, weight_grad, gain_grad, bias_grad)


def solution(mesh):
    return jax.shard_map(
        local,
        mesh=mesh,
        in_specs=(
            P(("shard", "rep"), None),
            P(),
            P(),
            P("shard", None),
            P(("shard", "rep"), None),
            P(),
        ),
        out_specs=(
            P(("shard", "rep"), None),
            P(("shard", "rep"), None),
            P("shard", None),
            P(),
            P(),
        ),
        check_vma=False,
    )
```

profile of v0, /device:TPU:16, one launch (start us, length us, event | category | flops | bytes accessed | tf_op | source)
XLA Modules:
  0.0 578.5 jit_solution(7815864115164983269)
XLA Ops:
  7.2 0.0 copy-start.6
  7.2 0.0 copy-start.3
  7.2 0.0 all-gather.2.cloned.1.call-start
  7.2 0.7 all-gather.2.cloned.1.call-update
  7.9 0.0 reduce-scatter.2.cloned.1.call-start
  8.0 6.3 %copy.12 = bf16[384,5120]{0,1:T(8,128)(2,1)} copy(bf16[384,5120]{1,0:T(8,128)(2,1)} %param.6) | data formatting | bytes 7864320 | tf_op args[0]
  14.2 0.0 copy-done.6
  14.2 0.7 scatter_custom_fusion
  15.0 3.0 fusion.7
  18.1 0.1 broadcast_bitcast_fusion.2
  18.1 0.1 broadcast_bitcast_fusion
  18.2 141.7 %all-gather.2.cloned.1.call-done = bf16[8192,1024]{1,0:T(8,128)(2,1)} async-done(((bf16[1024,1024]{1,0:T(8,128)(2,1)}), bf16[8192,1024]{1,0:T(8,128)(2,1)}) %all-gather.2.cloned.1.call-update) | async-done | bytes 16777232 | tf_op jit(solution)/shard_map/all_gather | solution.py:42
  160.0 0.0 copy-done.3
  160.0 12.9 %convolution_bitcast_fusion = f32[48,64,8,128]{3,2,1,0:T(8,128)} fusion(bf16[384,1024]{1,0:T(8,128)(2,1)S(1)} %copy-done.3, bf16[8192,1024]{1,0:T(8,128)(2,1)} %all-gather.2.cloned.1.call-done), kind=kOutput, calls=%fused_computation.24 | convolution fusion | flops 6442450944 | bytes 30146560 | tf_op jit(solution)/shard_map/dot_general | solution.py:45
  172.9 10.8 %copy.20 = f32[48,64,8,128]{3,2,0,1:T(8,128)} copy(f32[48,64,8,128]{3,2,1,0:T(8,128)} %convolution_bitcast_fusion) | data formatting | bytes 25165824 | tf_op jit(solution)/shard_map/reshape | solution.py:49
  183.7 8.7 %gather_fusion.1 = f32[40,384,128]{2,1,0:T(8,128)} fusion(f32[384,64,128]{2,0,1:T(8,128)} %bitcast.34, s32[1024]{0:T(1024)S(1)} %pad_clamp_fusion), kind=kCustom, calls=%fused_computation.1 | custom fusion | bytes 15728800 | tf_op jit(solution)/shard_map/jit(_take)/gather | solution.py:49
  192.4 0.0 copy-start.4
  192.4 9.1 %copy.16 = f32[384,40,128]{0,2,1:T(8,128)} copy(f32[384,40,128]{2,0,1:T(8,128)} %bitcast.35) | data formatting | bytes 15728640 | tf_op jit(solution)/shard_map/jit(_take)/gather | solution.py:49
  201.5 0.0 copy-done.4
  201.5 0.0 copy-start
  201.5 0.0 copy-start.1
  201.5 8.8 %fusion.10 = (f32[5120]{0:T(1024)S(1)}, f32[384]{0:T(512)S(1)}) fusion(bf16[384,5120]{0,1:T(8,128)(2,1)} %copy.12, f32[384,40,128]{0,2,1:T(8,128)} %copy.16, f32[384]{0:T(512)S(1)} %add_rsqrt_fusion, pred[5120]{0:T(1024)(128)(4,1)S(1)} %broadcast_bitcast_fusion.2, f32[5120]{0:T(1024)S(1)} %copy-done.4), kind=kLoop, calls=%fused_computation.19 | loop fusion | flops 15723136 | bytes 11845632 | tf_op jit(solution)/shard_map/reduce_sum | solution.py:65
  210.3 0.0 copy-done
  210.3 0.0 copy-done.1
  210.3 5.5 fusion.6
  215.8 6.3 %copy.13 = bf16[384,40,128]{2,0,1:T(8,128)(2,1)} copy(bf16[384,40,128]{0,2,1:T(8,128)(2,1)} %bitcast.37) | data formatting | bytes 7864320 | tf_op jit(solution)/shard_map/reshape | solution.py:38
  222.1 6.1 %gather_fusion = bf16[64,384,128]{2,1,0:T(8,128)(2,1)} fusion(bf16[384,40,128]{2,0,1:T(8,128)(2,1)} %copy.13, s32[1024]{0:T(1024)S(1)} %pad_clamp_fusion.1), kind=kCustom, calls=%fused_computation | custom fusion | bytes 12583168 | tf_op jit(solution)/shard_map/jit(_take)/gather | solution.py:39
  228.2 8.6 %copy.14 = bf16[384,64,128]{0,2,1:T(8,128)(2,1)} copy(bf16[384,64,128]{2,0,1:T(8,128)(2,1)} %bitcast.36) | data formatting | bytes 12582912 | tf_op jit(solution)/shard_map/jit(_take)/gather | solution.py:39
  236.8 6.9 %fusion.12 = bf16[384,8192]{0,1:T(8,128)(2,1)S(1)} fusion(bf16[384,64,128]{0,2,1:T(8,128)(2,1)} %copy.14, pred[8192]{0:T(1024)(128)(4,1)S(1)} %get-tuple-element.18, pred[8192]{0:T(1024)(128)(4,1)S(1)} %get-tuple-element.19), kind=kLoop, calls=%fused_computation.23 | loop fusion | flops 6291456 | bytes 12599296 | tf_op jit(solution)/shard_map/jit(_where)/select_n | solution.py:40
  243.7 0.0 copy-start.2
  243.7 2.6 copy-done.2
  246.3 11.7 %multiply_convert_fusion = bf16[8192,1024]{1,0:T(8,128)(2,1)} fusion(bf16[384,8192]{0,1:T(8,128)(2,1)S(1)} %fusion.12, bf16[384,1024]{1,0:T(8,128)(2,1)S(1)} %copy-done.3), kind=kOutput, calls=%fused_computation.3 | convolution fusion | flops 6459228160 | bytes 23855104 | tf_op jit(solution)/shard_map/dot_general | solution.py:56
  258.0 0.0 reduce-scatter.2.cloned.1.call-update
  258.0 0.0 copy-start.5
  258.0 0.1 convert_reduce_fusion
  258.2 6.3 %copy.17 = bf16[384,5120]{1,0:T(8,128)(2,1)} copy(bf16[384,5120]{0,1:T(8,128)(2,1)} %get-tuple-element.14) | data formatting | bytes 7864320
  264.4 42.3 %all-reduce = (f32[5120]{0:T(1024)}, f32[1024]{0:T(1024)}) all-reduce(f32[5120]{0:T(1024)S(1)} %broadcast_multiply_fusion, f32[1024]{0:T(1024)S(1)} %broadcast_multiply_fusion.1), channel_id=1, replica_groups=mesh['shard'=8,'rep'=4] {'shard','rep'}, use_global_device_ids=true, to_apply=%region_6.7 | all-reduce | flops 6144 | bytes 49152 | tf_op jit(solution)/shard_map/psum | solution.py:68
  306.7 0.0 copy-done.5
  306.7 13.0 %add_convert_fusion = bf16[384,1024]{1,0:T(8,128)(2,1)} fusion(bf16[384,8192]{0,1:T(8,128)(2,1)} %copy-done.2, bf16[8192,1024]{1,0:T(8,128)(2,1)} %all-gather.2.cloned.1.call-done, f32[1024]{0:T(1024)S(1)} %copy-done.5), kind=kOutput, calls=%fused_computation.26 | convolution fusion | flops 6443237376 | bytes 23859200 | tf_op jit(solution)/shard_map/dot_general | solution.py:44
  319.7 105.2 %reduce-scatter.2.cloned.1.call-done = bf16[1024,1024]{1,0:T(8,128)(2,1)} async-done(((bf16[8192,1024]{1,0:T(8,128)(2,1)}), bf16[1024,1024]{1,0:T(8,128)(2,1)}) %reduce-scatter.2.cloned.1.call-update) | async-done | bytes 2097168 | tf_op jit(solution)/shard_map/reduce_scatter | solution.py:54
  424.9 146.8 %all-reduce.2 = f32[1024,1024]{1,0:T(8,128)} all-reduce(bf16[1024,1024]{1,0:T(8,128)(2,1)} %reduce-scatter.2.cloned.1.call-done), channel_id=1, replica_groups=mesh['shard'=8,'rep'=4] {'rep'}, use_global_device_ids=true, to_apply=%region_4.5 | all-reduce | flops 1048576 | bytes 6291456 | tf_op jit(solution)/shard_map/psum | solution.py:67
  (11 shorter events, 0.1 us)
Async XLA Ops:
  7.2 7.1 %copy-start.6 = (s32[40]{0:T(128)S(1)}, s32[40]{0:T(128)}, u32[]{:S(2)}) copy-start(s32[40]{0:T(128)} %param.11) | copy-start | bytes 484
  7.2 152.8 %copy-start.3 = (bf16[384,1024]{1,0:T(8,128)(2,1)S(1)}, bf16[384,1024]{1,0:T(8,128)(2,1)}, u32[]{:S(2)}) copy-start(bf16[384,1024]{1,0:T(8,128)(2,1)} %param.10) | copy-start | bytes 2359300
  7.2 152.8 %all-gather.2.cloned.1.call-start = ((), (), s32[]{:S(2)}) async-start(), calls=%async_computation.1 | async-start | bytes 18874368 | tf_op jit(solution)/shard_map/all_gather | solution.py:42
  7.9 417.0 %reduce-scatter.2.cloned.1.call-start = ((), (), s32[]{:S(2)}) async-start(), calls=%async_computation.2 | async-start | bytes 18874368 | tf_op jit(solution)/shard_map/reduce_scatter | solution.py:54
  192.4 9.1 %copy-start.4 = (f32[5120]{0:T(1024)S(1)}, f32[5120]{0:T(1024)}, u32[]{:S(2)}) copy-start(f32[5120]{0:T(1024)} %param.7) | copy-start | bytes 61444
  201.5 8.8 %copy-start = (f32[384,40,128]{0,2,1:T(8,128)S(1)}, f32[384,40,128]{0,2,1:T(8,128)}, u32[]{:S(2)}) copy-start(f32[384,40,128]{0,2,1:T(8,128)} %copy.16) | copy-start | bytes 23592964
  201.5 8.8 %copy-start.1 = (bf16[384,5120]{0,1:T(8,128)(2,1)S(1)}, bf16[384,5120]{0,1:T(8,128)(2,1)}, u32[]{:S(2)}) copy-start(bf16[384,5120]{0,1:T(8,128)(2,1)} %copy.12) | copy-start | bytes 11796484
  243.7 2.6 copy-start.2
  258.0 48.7 %copy-start.5 = (f32[1024]{0:T(1024)S(1)}, f32[1024]{0:T(1024)}, u32[]{:S(2)}) copy-start(f32[1024]{0:T(1024)} %param.8) | copy-start | bytes 12292
Sparse Core Ops, SparseCore 0:
  9.6 150.3 all-gather.1
  258.1 166.7 reduce-scatter.1
where the time goes:
time: 580 us; the launch traced here: 579 us
  waiting for transfers between devices  248 us (43%)
  blocking collectives  189 us (33%)
  local copies, waits for them, and re-layouts  65.7 us (11%)
  matrix products  37.5 us (6%)
  other arithmetic  24.4 us (4%)
  between operations  14.2 us (2%)
    psum x1, blocking collectives, local(): weight_grad = lax.psum(group_sum, 'rep')  147 us
    all_gather x1, waiting for transfers between devices, local(): piece = lax.all_gather(key_weight, 'shard', axis=0, tiled=True)  142 us
    reduce_scatter x1, waiting for transfers between devices, local(): lax.psum_scatter((lax.dot_general(columns, cotangent, (((0,), (0,)), ((),...  105 us
    psum x1, blocking collectives, local(): gain_grad, bias_grad = lax.psum((gain_part, bias_part), ('shard', 'rep'))  42.3 us
    gather x2, local copies, waits for them, and re-layouts, local(): jnp.take(backward_part.reshape(row_count, slot_total, BLK), block_slot, a...  17.8 us
    unnamed x16, local copies, waits for them, and re-layouts  15.2 us
    gather x2, local copies, waits for them, and re-layouts, local(): jnp.take(normed_blocks, jnp.maximum(block_of_slot, 0), axis=1)  14.7 us
    dot_general x1, matrix products, local(): forward_sum = jnp.dot(columns, piece, preferred_element_type=jnp.float32)  13 us
  transfers between devices with their start and end apart: 2, of which 2 were waited for; matrix products, arithmetic and copies ran while one was open for 5% of the time, Pallas kernels for 0%

commit v1 on v0

--- a/solution.py
+++ b/solution.py
@@ -65,7 +65,7 @@
     gain_part = jnp.sum(grad_normed * values * inv_rms, axis=0) * grad_scale
     bias_part = jnp.sum(cotangent.astype(jnp.float32), axis=0) * grad_scale
     weight_grad = lax.psum(group_sum, "rep")
-    gain_grad, bias_grad = lax.psum((gain_part, bias_part), ("shard", "rep"))
+    gain_grad, bias_grad = lax.psum(lax.psum((gain_part, bias_part), "rep"), "shard")
     return (projected, token_grad, weight_grad, gain_grad, bias_grad)
 
 

time: 580 us -> 607 us (1.047); the launches traced: 579 us -> 598 us
  waiting for transfers between devices: 248 us -> 289 us
  blocking collectives: 189 us -> 168 us
    reduce_scatter x1, waiting for transfers between devices: 105 us -> 146 us  [local(): lax.psum_scatter((lax.dot_general(columns, cotangent, (((0,), (0,)), ((),...]
    psum x1, blocking collectives: 42.3 us -> 19.4 us  [local(): lax.psum(lax.psum((gain_part, bias_part), 'rep'), 'shard')]
where the time goes in v1:
time: 607 us; the launch traced here: 598 us
  waiting for transfers between devices  289 us (48%)
  blocking collectives  168 us (28%)
  local copies, waits for them, and re-layouts  65.7 us (11%)
  matrix products  37.7 us (6%)
  other arithmetic  24.4 us (4%)
  between operations  14.2 us (2%)
    psum x1, blocking collectives, local(): weight_grad = lax.psum(group_sum, 'rep')  148 us
    reduce_scatter x1, waiting for transfers between devices, local(): lax.psum_scatter((lax.dot_general(columns, cotangent, (((0,), (0,)), ((),...  146 us
    all_gather x1, waiting for transfers between devices, local(): piece = lax.all_gather(key_weight, 'shard', axis=0, tiled=True)  142 us
    psum x1, blocking collectives, local(): lax.psum(lax.psum((gain_part, bias_part), 'rep'), 'shard')  19.4 us
    gather x2, local copies, waits for them, and re-layouts, local(): jnp.take(backward_part.reshape(row_count, slot_total, BLK), block_slot, a...  17.8 us
    unnamed x16, local copies, waits for them, and re-layouts  15.2 us
    gather x2, local copies, waits for them, and re-layouts, local(): jnp.take(normed_blocks, jnp.maximum(block_of_slot, 0), axis=1)  14.7 us
    dot_general x1, matrix products, local(): forward_sum = jnp.dot(columns, piece, preferred_element_type=jnp.float32)  13.2 us
  transfers between devices with their start and end apart: 2, of which 2 were waited for; matrix products, arithmetic and copies ran while one was open for 5% of the time, Pallas kernels for 0%

profile of v1, /device:TPU:16, one launch (start us, length us, event | category | flops | bytes accessed | tf_op | source)
XLA Modules:
  0.0 598.5 jit_solution(10817399489784882773)
XLA Ops:
  7.2 0.0 copy-start.6
  7.2 0.0 copy-start.3
  7.2 0.0 all-gather.2.cloned.1.call-start
  7.2 0.7 all-gather.2.cloned.1.call-update
  7.9 0.0 reduce-scatter.2.cloned.1.call-start
  8.0 6.3 %copy.12 = bf16[384,5120]{0,1:T(8,128)(2,1)} copy(bf16[384,5120]{1,0:T(8,128)(2,1)} %param.6) | data formatting | bytes 7864320 | tf_op args[0]
  14.2 0.0 copy-done.6
  14.2 0.7 scatter_custom_fusion
  15.0 3.0 fusion.7
  18.1 0.1 broadcast_bitcast_fusion.2
  18.1 0.1 broadcast_bitcast_fusion
  18.2 141.7 %all-gather.2.cloned.1.call-done = bf16[8192,1024]{1,0:T(8,128)(2,1)} async-done(((bf16[1024,1024]{1,0:T(8,128)(2,1)}), bf16[8192,1024]{1,0:T(8,128)(2,1)}) %all-gather.2.cloned.1.call-update) | async-done | bytes 16777232 | tf_op jit(solution)/shard_map/all_gather | solution.py:42
  160.0 0.0 copy-done.3
  160.0 12.9 %convolution_bitcast_fusion = f32[48,64,8,128]{3,2,1,0:T(8,128)} fusion(bf16[384,1024]{1,0:T(8,128)(2,1)S(1)} %copy-done.3, bf16[8192,1024]{1,0:T(8,128)(2,1)} %all-gather.2.cloned.1.call-done), kind=kOutput, calls=%fused_computation.24 | convolution fusion | flops 6442450944 | bytes 30146560 | tf_op jit(solution)/shard_map/dot_general | solution.py:45
  172.9 10.8 %copy.20 = f32[48,64,8,128]{3,2,0,1:T(8,128)} copy(f32[48,64,8,128]{3,2,1,0:T(8,128)} %convolution_bitcast_fusion) | data formatting | bytes 25165824 | tf_op jit(solution)/shard_map/reshape | solution.py:49
  183.7 8.7 %gather_fusion.1 = f32[40,384,128]{2,1,0:T(8,128)} fusion(f32[384,64,128]{2,0,1:T(8,128)} %bitcast.34, s32[1024]{0:T(1024)S(1)} %pad_clamp_fusion), kind=kCustom, calls=%fused_computation.1 | custom fusion | bytes 15728800 | tf_op jit(solution)/shard_map/jit(_take)/gather | solution.py:49
  192.4 0.0 copy-start.4
  192.4 9.1 %copy.16 = f32[384,40,128]{0,2,1:T(8,128)} copy(f32[384,40,128]{2,0,1:T(8,128)} %bitcast.35) | data formatting | bytes 15728640 | tf_op jit(solution)/shard_map/jit(_take)/gather | solution.py:49
  201.5 0.0 copy-done.4
  201.5 0.0 copy-start
  201.5 0.0 copy-start.1
  201.5 8.8 %fusion.10 = (f32[5120]{0:T(1024)S(1)}, f32[384]{0:T(512)S(1)}) fusion(bf16[384,5120]{0,1:T(8,128)(2,1)} %copy.12, f32[384,40,128]{0,2,1:T(8,128)} %copy.16, f32[384]{0:T(512)S(1)} %add_rsqrt_fusion, pred[5120]{0:T(1024)(128)(4,1)S(1)} %broadcast_bitcast_fusion.2, f32[5120]{0:T(1024)S(1)} %copy-done.4), kind=kLoop, calls=%fused_computation.19 | loop fusion | flops 15723136 | bytes 11845632 | tf_op jit(solution)/shard_map/reduce_sum | solution.py:65
  210.3 0.0 copy-done
  210.3 0.0 copy-done.1
  210.3 5.5 fusion.6
  215.8 6.3 %copy.13 = bf16[384,40,128]{2,0,1:T(8,128)(2,1)} copy(bf16[384,40,128]{0,2,1:T(8,128)(2,1)} %bitcast.37) | data formatting | bytes 7864320 | tf_op jit(solution)/shard_map/reshape | solution.py:38
  222.1 6.1 %gather_fusion = bf16[64,384,128]{2,1,0:T(8,128)(2,1)} fusion(bf16[384,40,128]{2,0,1:T(8,128)(2,1)} %copy.13, s32[1024]{0:T(1024)S(1)} %pad_clamp_fusion.1), kind=kCustom, calls=%fused_computation | custom fusion | bytes 12583168 | tf_op jit(solution)/shard_map/jit(_take)/gather | solution.py:39
  228.2 8.6 %copy.14 = bf16[384,64,128]{0,2,1:T(8,128)(2,1)} copy(bf16[384,64,128]{2,0,1:T(8,128)(2,1)} %bitcast.36) | data formatting | bytes 12582912 | tf_op jit(solution)/shard_map/jit(_take)/gather | solution.py:39
  236.8 6.9 %fusion.12 = bf16[384,8192]{0,1:T(8,128)(2,1)S(1)} fusion(bf16[384,64,128]{0,2,1:T(8,128)(2,1)} %copy.14, pred[8192]{0:T(1024)(128)(4,1)S(1)} %get-tuple-element.21, pred[8192]{0:T(1024)(128)(4,1)S(1)} %get-tuple-element.22), kind=kLoop, calls=%fused_computation.23 | loop fusion | flops 6291456 | bytes 12599296 | tf_op jit(solution)/shard_map/jit(_where)/select_n | solution.py:40
  243.7 0.0 copy-start.2
  243.7 2.6 copy-done.2
  246.3 11.7 %multiply_convert_fusion = bf16[8192,1024]{1,0:T(8,128)(2,1)} fusion(bf16[384,8192]{0,1:T(8,128)(2,1)S(1)} %fusion.12, bf16[384,1024]{1,0:T(8,128)(2,1)S(1)} %copy-done.3), kind=kOutput, calls=%fused_computation.3 | convolution fusion | flops 6459228160 | bytes 23855104 | tf_op jit(solution)/shard_map/dot_general | solution.py:56
  258.0 0.0 reduce-scatter.2.cloned.1.call-update
  258.0 0.0 copy-start.5
  258.0 0.1 convert_reduce_fusion
  258.2 6.3 %copy.17 = bf16[384,5120]{1,0:T(8,128)(2,1)} copy(bf16[384,5120]{0,1:T(8,128)(2,1)} %get-tuple-element.17) | data formatting | bytes 7864320
  264.4 0.0 copy-done.5
  264.4 13.2 %add_convert_fusion = bf16[384,1024]{1,0:T(8,128)(2,1)} fusion(bf16[384,8192]{0,1:T(8,128)(2,1)} %copy-done.2, bf16[8192,1024]{1,0:T(8,128)(2,1)} %all-gather.2.cloned.1.call-done, f32[1024]{0:T(1024)S(1)} %copy-done.5), kind=kOutput, calls=%fused_computation.26 | convolution fusion | flops 6443237376 | bytes 23859200 | tf_op jit(solution)/shard_map/dot_general | solution.py:44
  277.6 146.2 %reduce-scatter.2.cloned.1.call-done = bf16[1024,1024]{1,0:T(8,128)(2,1)} async-done(((bf16[8192,1024]{1,0:T(8,128)(2,1)}), bf16[1024,1024]{1,0:T(8,128)(2,1)}) %reduce-scatter.2.cloned.1.call-update) | async-done | bytes 2097168 | tf_op jit(solution)/shard_map/reduce_scatter | solution.py:54
  423.9 148.4 %all-reduce.3 = (f32[1024,1024]{1,0:T(8,128)}, f32[5120]{0:T(1024)S(1)}, f32[1024]{0:T(1024)S(1)}) all-reduce(bf16[1024,1024]{1,0:T(8,128)(2,1)} %reduce-scatter.2.cloned.1.call-done, f32[5120]{0:T(1024)S(1)} %broadcast_multiply_fusion, f32[1024]{0:T(1024)S(1)} %broadcast_multiply_fusion.1), channel_id=1, replica_groups=mesh['shard'=8,'rep'=4] {'rep'}, use_global_device_ids=true, to_apply=%region_4.5 | all-reduce | flops 1054720 | bytes 6340608 | tf_op jit(solution)/shard_map/psum | solution.py:67
  572.3 19.4 %all-reduce = (f32[5120]{0:T(1024)}, f32[1024]{0:T(1024)}) all-reduce(f32[5120]{0:T(1024)S(1)} %get-tuple-element.15, f32[1024]{0:T(1024)S(1)} %get-tuple-element.16), channel_id=1, replica_groups=mesh['shard'=8,'rep'=4] {'shard'}, use_global_device_ids=true, to_apply=%region_7.8 | all-reduce | flops 6144 | bytes 49152 | tf_op jit(solution)/shard_map/psum | solution.py:68
  (11 shorter events, 0.1 us)
Async XLA Ops:
  7.2 7.1 %copy-start.6 = (s32[40]{0:T(128)S(1)}, s32[40]{0:T(128)}, u32[]{:S(2)}) copy-start(s32[40]{0:T(128)} %param.11) | copy-start | bytes 484
  7.2 152.8 %copy-start.3 = (bf16[384,1024]{1,0:T(8,128)(2,1)S(1)}, bf16[384,1024]{1,0:T(8,128)(2,1)}, u32[]{:S(2)}) copy-start(bf16[384,1024]{1,0:T(8,128)(2,1)} %param.10) | copy-start | bytes 2359300
  7.2 152.8 %all-gather.2.cloned.1.call-start = ((), (), s32[]{:S(2)}) async-start(), calls=%async_computation.1 | async-start | bytes 18874368 | tf_op jit(solution)/shard_map/all_gather | solution.py:42
  7.9 415.9 %reduce-scatter.2.cloned.1.call-start = ((), (), s32[]{:S(2)}) async-start(), calls=%async_computation.2 | async-start | bytes 18874368 | tf_op jit(solution)/shard_map/reduce_scatter | solution.py:54
  192.4 9.1 %copy-start.4 = (f32[5120]{0:T(1024)S(1)}, f32[5120]{0:T(1024)}, u32[]{:S(2)}) copy-start(f32[5120]{0:T(1024)} %param.7) | copy-start | bytes 61444
  201.5 8.8 %copy-start = (f32[384,40,128]{0,2,1:T(8,128)S(1)}, f32[384,40,128]{0,2,1:T(8,128)}, u32[]{:S(2)}) copy-start(f32[384,40,128]{0,2,1:T(8,128)} %copy.16) | copy-start | bytes 23592964
  201.5 8.8 %copy-start.1 = (bf16[384,5120]{0,1:T(8,128)(2,1)S(1)}, bf16[384,5120]{0,1:T(8,128)(2,1)}, u32[]{:S(2)}) copy-start(bf16[384,5120]{0,1:T(8,128)(2,1)} %copy.12) | copy-start | bytes 11796484
  243.7 2.6 copy-start.2
  258.0 6.4 %copy-start.5 = (f32[1024]{0:T(1024)S(1)}, f32[1024]{0:T(1024)}, u32[]{:S(2)}) copy-start(f32[1024]{0:T(1024)} %param.8) | copy-start | bytes 12292
Sparse Core Ops, SparseCore 0:
  9.6 150.3 all-gather.1
  258.1 165.6 reduce-scatter.1
